TPU v7x, 32 devices: a whole 2x2x4 slice. The times are simulated.
32 devices in a mesh: dp: 4 (over y, x), ctx: 8 (over z, core).
Axes of the slice: x: 2, y: 2, z: 4, core: 2. Of those that a mesh axis runs over, the one named last changes fastest.
Arguments:
- inputs: bfloat16 [4, 16, 128, 2048], P('dp', 'ctx'), may hold values from -6 to 6
- block_of: int32 [4, 16], P('dp', 'ctx'), may hold values from 0 to 15, as said below
- first_gain: float32 [2048], P('dp'), may hold values from 0.5 to 1.5
- first_shift: float32 [2048], P('dp'), may hold values from -3 to 3
- w_qkv: bfloat16 [2048, 6144], P('dp'), may hold values from -8 to 8
- qkv_bias: float32 [6144], P('dp'), may hold values from -3 to 3
- w_out: bfloat16 [2048, 2048], P('dp'), may hold values from -0.75 to 0.75
- second_gain: float32 [2048], P('dp'), may hold values from 0.5 to 1.5
- second_shift: float32 [2048], P('dp'), may hold values from -3 to 3
- w_gateup: bfloat16 [2048, 11264], P('dp'), may hold values from -0.125 to 0.125
- w_down: bfloat16 [5632, 2048], P('dp'), may hold values from -0.078125 to 0.078125
- cotangent: bfloat16 [4, 16, 128, 2048], P('dp', 'ctx'), may hold values from -6 to 6
Outputs:
- outputs: bfloat16 [4, 16, 128, 2048], P('dp', 'ctx')
- grad_inputs: float32 [4, 16, 128, 2048], P('dp', 'ctx')
- grad_first_gain: float32 [2048], P('dp')
- grad_first_shift: float32 [2048], P('dp')
- grad_w_qkv: float32 [2048, 6144], P('dp')
- grad_qkv_bias: float32 [6144], P('dp')
- grad_w_out: float32 [2048, 2048], P('dp')
- grad_second_gain: float32 [2048], P('dp')
- grad_second_shift: float32 [2048], P('dp')
- grad_w_gateup: float32 [2048, 11264], P('dp')
- grad_w_down: float32 [5632, 2048], P('dp')
Inputs may be any that keep to these rules, and one draw needn't show every extreme that they name: `block_of`: for each sequence the 16 entries are a permutation of the blocks, and the two slots of one index of ctx hold blocks b and 15 - b, in either order.
All inputs are finite; a program needn't handle non-finite values.
Results may differ from a plain program's by a relative error of at most 0.035.
Values may be sent and summed in bfloat16 or wider, within the bound.
A program may use at most 640 MiB of HBM per device.

v0:
```python
import jax
import jax.numpy as jnp
from jax import lax
from jax.sharding import PartitionSpec as P

HEADS = 32
HEAD_DIM = 64
ROT = 16
epsilon = 1e-05


def layer_norm(token_rows, gain_vec, shift_vec):
    centre = jnp.mean(token_rows, axis=-1, keepdims=True)
    centred = token_rows - centre
    spread = jnp.mean(centred * centred, axis=-1, keepdims=True)
    inverse = lax.rsqrt(spread + epsilon)
    normed = centred * inverse
    return (normed * gain_vec + shift_vec, normed, inverse)


def norm_back(grad_rows, normed, inverse, gain_vec):
    scaled = grad_rows * gain_vec
    mean_plain = jnp.mean(scaled, axis=-1, keepdims=True)
    mean_cross = jnp.mean(scaled * normed, axis=-1, keepdims=True)
    return inverse * (scaled - mean_plain - normed * mean_cross)


def rotary_tables(positions):
    half_rot = ROT // 2
    frequency = 10000.0 ** (-2.0 * jnp.arange(half_rot, dtype=jnp.float32) / ROT)
    angles = positions.astype(jnp.float32)[:, None] * frequency[None, :]
    return (jnp.cos(angles), jnp.sin(angles))


def rotate_heads(head_rows, cosine, sine_part, direction_sign):
    half_rot = ROT // 2
    first_half = head_rows[..., :half_rot]
    second_half = head_rows[..., half_rot:ROT]
    cos_rows = cosine[:, None, :]
    sin_rows = sine_part[:, None, :] * direction_sign
    return jnp.concatenate(
        [
            first_half * cos_rows - second_half * sin_rows,
            second_half * cos_rows + first_half * sin_rows,
            head_rows[..., ROT:],
        ],
        axis=-1,
    )


def attend(query, keys_all, values_all, query_pos, key_pos):
    tok_count, head_count, head_width = query.shape
    per_group = min(4, head_count)
    score_scale = head_width ** (-0.5)
    allowed = key_pos[None, :] <= query_pos[:, None]

    def group_step(group_index, carry):
        output_all, lse_all = carry
        first_head = jnp.asarray(group_index).astype(jnp.int32) * per_group
        query_part = lax.dynamic_slice_in_dim(query, first_head, per_group, 1)
        keys_part = lax.dynamic_slice_in_dim(keys_all, first_head, per_group, 1)
        values_part = lax.dynamic_slice_in_dim(values_all, first_head, per_group, 1)
        scores = (
            jnp.einsum("thd,shd->hts", query_part, keys_part, preferred_element_type=jnp.float32)
            * score_scale
        )
        scores = jnp.where(allowed[None], scores, -jnp.inf)
        row_max = jnp.max(scores, axis=-1, keepdims=True)
        log_total = row_max + jnp.log(jnp.sum(jnp.exp(scores - row_max), axis=-1, keepdims=True))
        weights = jnp.exp(scores - log_total).astype(jnp.bfloat16)
        mixed = jnp.einsum(
            "hts,shd->thd", weights, values_part, preferred_element_type=jnp.float32
        ).astype(jnp.bfloat16)
        output_all = lax.dynamic_update_slice_in_dim(output_all, mixed, first_head, 1)
        lse_all = lax.dynamic_update_slice_in_dim(lse_all, log_total[..., 0], first_head, 0)
        return (output_all, lse_all)

    init = (jnp.zeros(query.shape, jnp.bfloat16), jnp.zeros((head_count, tok_count), jnp.float32))
    return lax.fori_loop(0, head_count // per_group, group_step, init)


def attend_back(query, keys_all, values_all, output, grad_output, lse_all, query_pos, key_pos):
    tok_count, head_count, head_width = query.shape
    per_group = min(4, head_count)
    score_scale = head_width ** (-0.5)
    allowed = key_pos[None, :] <= query_pos[:, None]
    delta_all = jnp.einsum(
        "thd,thd->ht", output.astype(jnp.float32), grad_output.astype(jnp.float32)
    )

    def group_step(group_index, carry):
        grad_q_all, grad_k_all, grad_v_all = carry
        first_head = jnp.asarray(group_index).astype(jnp.int32) * per_group
        query_part = lax.dynamic_slice_in_dim(query, first_head, per_group, 1)
        keys_part = lax.dynamic_slice_in_dim(keys_all, first_head, per_group, 1)
        values_part = lax.dynamic_slice_in_dim(values_all, first_head, per_group, 1)
        dout_part = lax.dynamic_slice_in_dim(grad_output, first_head, per_group, 1)
        lse_part = lax.dynamic_slice_in_dim(lse_all, first_head, per_group, 0)
        delta_part = lax.dynamic_slice_in_dim(delta_all, first_head, per_group, 0)
        scores = (
            jnp.einsum("thd,shd->hts", query_part, keys_part, preferred_element_type=jnp.float32)
            * score_scale
        )
        scores = jnp.where(allowed[None], scores, -jnp.inf)
        probs = jnp.exp(scores - lse_part[..., None])
        probs_low = probs.astype(jnp.bfloat16)
        grad_v_part = jnp.einsum(
            "hts,thd->shd", probs_low, dout_part, preferred_element_type=jnp.float32
        )
        grad_p = jnp.einsum(
            "thd,shd->hts", dout_part, values_part, preferred_element_type=jnp.float32
        )
        grad_s = (probs * (grad_p - delta_part[..., None])).astype(jnp.bfloat16)
        grad_q_part = (
            jnp.einsum("hts,shd->thd", grad_s, keys_part, preferred_element_type=jnp.float32)
            * score_scale
        )
        grad_k_part = (
            jnp.einsum("hts,thd->shd", grad_s, query_part, preferred_element_type=jnp.float32)
            * score_scale
        )
        grad_q_all = lax.dynamic_update_slice_in_dim(grad_q_all, grad_q_part, first_head, 1)
        grad_k_all = lax.dynamic_update_slice_in_dim(grad_k_all, grad_k_part, first_head, 1)
        grad_v_all = lax.dynamic_update_slice_in_dim(grad_v_all, grad_v_part, first_head, 1)
        return (grad_q_all, grad_k_all, grad_v_all)

    init = (
        jnp.zeros(query.shape, jnp.float32),
        jnp.zeros(keys_all.shape, jnp.float32),
        jnp.zeros(values_all.shape, jnp.float32),
    )
    return lax.fori_loop(0, head_count // per_group, group_step, init)


def local(
    inputs,
    block_of,
    first_gain,
    first_shift,
    w_qkv,
    qkv_bias,
    w_out,
    second_gain,
    second_shift,
    w_gateup,
    w_down,
    cotangent,
):
    block_rows = inputs.shape[2]
    tok_count = inputs.shape[1] * block_rows
    model_width = inputs.shape[3]
    token_rows = inputs.reshape(tok_count, model_width).astype(jnp.float32)
    offsets = jnp.arange(block_rows, dtype=jnp.int32)
    local_pos = (block_of.reshape(-1)[:, None] * block_rows + offsets[None, :]).reshape(tok_count)
    cosine, sine_part = rotary_tables(local_pos)
    head_shape = (tok_count, HEADS, HEAD_DIM)
    full_qkv, full_out, gain_one, shift_one, bias_full = (
        lax.all_gather(w_qkv, "dp", axis=0, tiled=True),
        lax.all_gather(w_out, "dp", axis=0, tiled=True),
        lax.all_gather(first_gain.astype(jnp.bfloat16), "dp", axis=0, tiled=True).astype(
            first_gain.dtype
        ),
        lax.all_gather(first_shift.astype(jnp.bfloat16), "dp", axis=0, tiled=True).astype(
            first_shift.dtype
        ),
        lax.all_gather(qkv_bias.astype(jnp.bfloat16), "dp", axis=0, tiled=True).astype(
            qkv_bias.dtype
        ),
    )
    normed_out, normed_one, inverse_one = layer_norm(token_rows, gain_one, shift_one)
    hidden_one = normed_out.astype(jnp.bfloat16)
    projected = jnp.dot(hidden_one, full_qkv, preferred_element_type=jnp.float32) + bias_full
    query = rotate_heads(
        projected[:, :model_width].reshape(head_shape), cosine, sine_part, 1.0
    ).astype(jnp.bfloat16)
    keys_flat = (
        rotate_heads(
            projected[:, model_width : 2 * model_width].reshape(head_shape), cosine, sine_part, 1.0
        )
        .reshape(tok_count, model_width)
        .astype(jnp.bfloat16)
    )
    values_flat = projected[:, 2 * model_width :].astype(jnp.bfloat16)
    keys_gathered, values_gathered, blocks_gathered = (
        lax.all_gather(keys_flat, "ctx", axis=0, tiled=True),
        lax.all_gather(values_flat, "ctx", axis=0, tiled=True),
        lax.all_gather(block_of, "ctx", axis=1, tiled=True),
    )
    seq_rows = keys_gathered.shape[0]
    key_pos = (blocks_gathered.reshape(-1)[:, None] * block_rows + offsets[None, :]).reshape(
        seq_rows
    )
    key_shape = (seq_rows, HEADS, HEAD_DIM)
    attended, log_totals = attend(
        query,
        keys_gathered.reshape(key_shape),
        values_gathered.reshape(key_shape),
        local_pos,
        key_pos,
    )
    attended_flat = attended.reshape(tok_count, model_width)
    middle = token_rows + jnp.dot(attended_flat, full_out, preferred_element_type=jnp.float32)
    full_gateup, full_down, gain_two, shift_two = (
        lax.all_gather(w_gateup, "dp", axis=0, tiled=True),
        lax.all_gather(w_down, "dp", axis=0, tiled=True),
        lax.all_gather(second_gain.astype(jnp.bfloat16), "dp", axis=0, tiled=True).astype(
            second_gain.dtype
        ),
        lax.all_gather(second_shift.astype(jnp.bfloat16), "dp", axis=0, tiled=True).astype(
            second_shift.dtype
        ),
    )
    normed_out_two, normed_two, inverse_two = layer_norm(middle, gain_two, shift_two)
    hidden_two = normed_out_two.astype(jnp.bfloat16)
    gate_up = jnp.dot(hidden_two, full_gateup, preferred_element_type=jnp.float32)
    hidden_units = full_down.shape[0]
    gate_part = gate_up[:, :hidden_units]
    up_part = gate_up[:, hidden_units:]
    sigmoid_gate = jax.nn.sigmoid(gate_part)
    activation = (gate_part * sigmoid_gate * up_part).astype(jnp.bfloat16)
    result = middle + jnp.dot(activation, full_down, preferred_element_type=jnp.float32)
    outputs = result.astype(jnp.bfloat16).reshape(inputs.shape)
    grad_rows = cotangent.reshape(tok_count, model_width)
    grad_act = jnp.einsum("td,fd->tf", grad_rows, full_down, preferred_element_type=jnp.float32)
    grad_gate = grad_act * up_part * sigmoid_gate * (1.0 + gate_part * (1.0 - sigmoid_gate))
    grad_up = grad_act * gate_part * sigmoid_gate
    grad_gu = jnp.concatenate([grad_gate, grad_up], axis=1).astype(jnp.bfloat16)
    grad_hidden_two = jnp.einsum(
        "tf,df->td", grad_gu, full_gateup, preferred_element_type=jnp.float32
    )
    gain_two_term = jnp.sum(grad_hidden_two * normed_two, axis=0)
    shift_two_term = jnp.sum(grad_hidden_two, axis=0)
    grad_middle = grad_rows.astype(jnp.float32) + norm_back(
        grad_hidden_two, normed_two, inverse_two, gain_two
    )
    grad_gateup = jnp.einsum("td,tf->df", hidden_two, grad_gu, preferred_element_type=jnp.float32)
    grad_down = jnp.einsum("tf,td->fd", activation, grad_rows, preferred_element_type=jnp.float32)
    mlp_shards = (
        lax.psum_scatter(
            grad_gateup.astype(jnp.bfloat16), "dp", scatter_dimension=0, tiled=True
        ).astype(jnp.float32),
        lax.psum_scatter(
            grad_down.astype(jnp.bfloat16), "dp", scatter_dimension=0, tiled=True
        ).astype(jnp.float32),
        lax.psum_scatter(
            gain_two_term.astype(jnp.bfloat16), "dp", scatter_dimension=0, tiled=True
        ).astype(jnp.float32),
        lax.psum_scatter(
            shift_two_term.astype(jnp.bfloat16), "dp", scatter_dimension=0, tiled=True
        ).astype(jnp.float32),
    )
    mlp_grads = (
        lax.psum(mlp_shards[0].astype(jnp.bfloat16), "ctx").astype(jnp.float32),
        lax.psum(mlp_shards[1].astype(jnp.bfloat16), "ctx").astype(jnp.float32),
        lax.psum(mlp_shards[2].astype(jnp.bfloat16), "ctx").astype(jnp.float32),
        lax.psum(mlp_shards[3].astype(jnp.bfloat16), "ctx").astype(jnp.float32),
    )
    full_qkv_again, full_out_again, gain_again = (
        lax.all_gather(w_qkv, "dp", axis=0, tiled=True),
        lax.all_gather(w_out, "dp", axis=0, tiled=True),
        lax.all_gather(first_gain.astype(jnp.bfloat16), "dp", axis=0, tiled=True).astype(
            first_gain.dtype
        ),
    )
    grad_middle_low = grad_middle.astype(jnp.bfloat16)
    grad_attended = jnp.einsum(
        "te,de->td", grad_middle_low, full_out_again, preferred_element_type=jnp.float32
    ).astype(jnp.bfloat16)
    grad_query, grad_keys_all, grad_values_all = attend_back(
        query,
        keys_gathered.reshape(key_shape),
        values_gathered.reshape(key_shape),
        attended,
        grad_attended.reshape(head_shape),
        log_totals,
        local_pos,
        key_pos,
    )
    grad_keys, grad_values = (
        lax.psum_scatter(
            grad_keys_all.reshape(seq_rows, model_width).astype(jnp.bfloat16),
            "ctx",
            scatter_dimension=0,
            tiled=True,
        ).astype(jnp.float32),
        lax.psum_scatter(
            grad_values_all.reshape(seq_rows, model_width).astype(jnp.bfloat16),
            "ctx",
            scatter_dimension=0,
            tiled=True,
        ).astype(jnp.float32),
    )
    grad_query_plain = rotate_heads(grad_query, cosine, sine_part, -1.0).reshape(
        tok_count, model_width
    )
    grad_keys_plain = rotate_heads(grad_keys.reshape(head_shape), cosine, sine_part, -1.0).reshape(
        tok_count, model_width
    )
    grad_proj = jnp.concatenate([grad_query_plain, grad_keys_plain, grad_values], axis=1)
    grad_proj_low = grad_proj.astype(jnp.bfloat16)
    grad_hidden_one = jnp.einsum(
        "tf,df->td", grad_proj_low, full_qkv_again, preferred_element_type=jnp.float32
    )
    bias_term = jnp.sum(grad_proj, axis=0)
    gain_one_term = jnp.sum(grad_hidden_one * normed_one, axis=0)
    shift_one_term = jnp.sum(grad_hidden_one, axis=0)
    grad_inputs = grad_middle + norm_back(grad_hidden_one, normed_one, inverse_one, gain_again)
    grad_wout = jnp.einsum(
        "td,te->de", attended_flat, grad_middle_low, preferred_element_type=jnp.float32
    )
    grad_wqkv = jnp.einsum(
        "td,tf->df", hidden_one, grad_proj_low, preferred_element_type=jnp.float32
    )
    attn_shards = (
        lax.psum_scatter(
            grad_wqkv.astype(jnp.bfloat16), "dp", scatter_dimension=0, tiled=True
        ).astype(jnp.float32),
        lax.psum_scatter(
            bias_term.astype(jnp.bfloat16), "dp", scatter_dimension=0, tiled=True
        ).astype(jnp.float32),
        lax.psum_scatter(
            grad_wout.astype(jnp.bfloat16), "dp", scatter_dimension=0, tiled=True
        ).astype(jnp.float32),
        lax.psum_scatter(
            gain_one_term.astype(jnp.bfloat16), "dp", scatter_dimension=0, tiled=True
        ).astype(jnp.float32),
        lax.psum_scatter(
            shift_one_term.astype(jnp.bfloat16), "dp", scatter_dimension=0, tiled=True
        ).astype(jnp.float32),
    )
    attn_grads = (
        lax.psum(attn_shards[0].astype(jnp.bfloat16), "ctx").astype(jnp.float32),
        lax.psum(attn_shards[1].astype(jnp.bfloat16), "ctx").astype(jnp.float32),
        lax.psum(attn_shards[2].astype(jnp.bfloat16), "ctx").astype(jnp.float32),
        lax.psum(attn_shards[3].astype(jnp.bfloat16), "ctx").astype(jnp.float32),
        lax.psum(attn_shards[4].astype(jnp.bfloat16), "ctx").astype(jnp.float32),
    )
    results = (
        attn_grads[3],
        attn_grads[4],
        attn_grads[0],
        attn_grads[1],
        attn_grads[2],
        mlp_grads[2],
        mlp_grads[3],
        mlp_grads[0],
        mlp_grads[1],
    )
    return (outputs, grad_inputs.reshape(inputs.shape)) + results


def solution(mesh):
    placed = (
        P("dp", "ctx", None, None),
        P("dp", "ctx"),
        P("dp"),
        P("dp"),
        P("dp", None),
        P("dp"),
        P("dp", None),
        P("dp"),
        P("dp"),
        P("dp", None),
        P("dp", None),
        P("dp", "ctx", None, None),
    )
    return jax.shard_map(
        local,
        mesh=mesh,
        in_specs=placed,
        out_specs=(
            P("dp", "ctx", None, None),
            P("dp", "ctx", None, None),
            P("dp"),
            P("dp"),
            P("dp", None),
            P("dp"),
            P("dp", None),
            P("dp"),
            P("dp"),
            P("dp", None),
            P("dp", None),
        ),
        check_vma=False,
    )
```

profile of v0, /device:TPU:0, one launch (start us, length us, event | category | flops | bytes accessed | tf_op | source)
XLA Modules:
  0.0 2973.1 jit_solution(4743477724046858579)
XLA Ops:
  8.0 9.6 all-gather.1
  17.7 8.1 all-gather
  25.8 7.6 all-gather.2
  34.6 205.7 %all-gather.12.cloned.1.call-done = bf16[2048,6144]{1,0:T(8,128)(2,1)} async-done(((bf16[512,6144]{1,0:T(8,128)(2,1)}), bf16[2048,6144]{1,0:T(8,128)(2,1)}) %all-gather.12.cloned.1.call-update) | async-done | bytes 25165840 | tf_op jit(solution)/shard_map/all_gather | solution.py:158
  240.3 11.6 convolution_add_fusion
  271.3 8.2 all-gather.4
  279.5 7.0 all-gather.3
  287.9 9.8 all-reduce
  299.5 38.6 %all-gather.14.cloned.1.call-done = bf16[2048,2048]{1,0:T(8,128)(2,1)} async-done(((bf16[256,2048]{1,0:T(8,128)(2,1)}), bf16[2048,2048]{1,0:T(8,128)(2,1)}) %all-gather.14.cloned.1.call-update) | async-done | bytes 8388624 | tf_op jit(solution)/shard_map/all_gather | solution.py:186
  338.1 12.3 copy.38
  350.4 70.9 %all-gather.16.cloned.1.call-done = bf16[2048,2048]{0,1:T(8,128)(2,1)} async-done(((bf16[256,2048]{0,1:T(8,128)(2,1)}), bf16[2048,2048]{0,1:T(8,128)(2,1)}) %all-gather.16.cloned.1.call-update) | async-done | bytes 8388624 | tf_op jit(solution)/shard_map/all_gather | solution.py:185
  421.5 72.2 %while.34 = (s32[]{:T(128)}, bf16[256,32,64]{0,2,1:T(8,128)(2,1)S(1)}, f32[32,256]{1,0:T(8,128)S(1)}, bf16[2048,32,64]{0,2,1:T(8,128)(2,1)}, bf16[256,32,64]{0,2...) while((s32[]{:T(128)}, ...), condition=%wide.region_5.6_spmd.clone, body=%wide.region_2.5_spmd.clone.sunk | while | flops 560528384 | bytes 29666480 | solution.py:79
  493.7 15.1 all-gather.18.cloned.1.call-done
  508.7 6.2 fusion.64
  515.3 397.2 %all-gather.20.cloned.1.call-done = bf16[2048,11264]{1,0:T(8,128)(2,1)} async-done(((bf16[512,11264]{1,0:T(8,128)(2,1)}), bf16[2048,11264]{1,0:T(8,128)(2,1)}) %all-gather.20.cloned.1.call-update) | async-done | bytes 46137360 | tf_op jit(solution)/shard_map/all_gather | solution.py:204
  912.5 28.4 fusion.62
  940.9 183.7 %all-gather.22.cloned.1.call-done = bf16[5632,2048]{1,0:T(8,128)(2,1)} async-done(((bf16[1408,2048]{1,0:T(8,128)(2,1)}), bf16[5632,2048]{1,0:T(8,128)(2,1)}) %all-gather.22.cloned.1.call-update) | async-done | bytes 23068688 | tf_op jit(solution)/shard_map/all_gather | solution.py:205
  1124.5 26.0 multiply_convert_fusion.2
  1150.6 22.1 multiply_reduce_fusion
  1176.4 6.8 convolution_convert_fusion.4
  1188.7 4.5 broadcast.231
  1197.5 142.9 %while.35 = (s32[]{:T(128)}, f32[256,32,64]{0,2,1:T(8,128)}, bf16[2048,32,64]{0,2,1:T(8,128)(2,1)}, bf16[2048,32,64]{0,2,1:T(8,128)(2,1)}, bf16[2048,32,64]{0,2,...) while((s32[]{:T(128)}, f32[256,32,64]{0,2,1:T(8,128)}, ...), condition=%wide.region_11.12_spmd.clone, body=%wide.region_10.11_spmd.clone.sunk | while | flops 1364262912 | bytes 47491280 | solution.py:132
  1200.7 4.5 multiply_convert_fusion.5
  1218.6 4.5 multiply_convert_fusion.5
  1236.4 4.5 multiply_convert_fusion.5
  1254.2 4.5 multiply_convert_fusion.5
  1272.1 4.5 multiply_convert_fusion.5
  1289.9 4.5 multiply_convert_fusion.5
  1307.7 4.5 multiply_convert_fusion.5
  1325.5 4.5 multiply_convert_fusion.5
  1341.2 7.5 convolution_convert_fusion.3
  1349.9 13.4 convolution_convert_fusion.1
  1366.2 63.9 %reduce-scatter.7.cloned.1.call-done = bf16[256,2048]{0,1:T(8,128)(2,1)} async-done(((bf16[2048,2048]{0,1:T(8,128)(2,1)}), bf16[256,2048]{0,1:T(8,128)(2,1)}) %reduce-scatter.7.cloned.1.call-update) | async-done | bytes 1048592 | tf_op jit(solution)/shard_map/reduce_scatter | solution.py:280
  1434.3 86.1 %reduce-scatter.9.cloned.1.call-done = bf16[256,2048]{0,1:T(8,128)(2,1)} async-done(((bf16[2048,2048]{0,1:T(8,128)(2,1)}), bf16[256,2048]{0,1:T(8,128)(2,1)}) %reduce-scatter.9.cloned.1.call-update) | async-done | bytes 1048592 | tf_op jit(solution)/shard_map/reduce_scatter | solution.py:286
  1527.2 13.6 convolution_convert_fusion.2
  1541.5 21.6 convolution_convert_fusion
  1563.2 45.7 %reduce-scatter.13.cloned.1.call-done = bf16[512,2048]{1,0:T(8,128)(2,1)} async-done(((bf16[2048,2048]{1,0:T(8,128)(2,1)}), bf16[512,2048]{1,0:T(8,128)(2,1)}) %reduce-scatter.13.cloned.1.call-update) | async-done | bytes 2097168 | tf_op jit(solution)/shard_map/reduce_scatter | solution.py:321
  1608.9 208.3 %reduce-scatter.17.cloned.1.call-done = bf16[1408,2048]{1,0:T(8,128)(2,1)} async-done(((bf16[5632,2048]{1,0:T(8,128)(2,1)}), bf16[1408,2048]{1,0:T(8,128)(2,1)}) %reduce-scatter.17.cloned.1.call-update) | async-done | bytes 5767184 | tf_op jit(solution)/shard_map/reduce_scatter | solution.py:242
  1817.2 224.9 %reduce-scatter.11.cloned.1.call-done = bf16[512,6144]{1,0:T(8,128)(2,1)} async-done(((bf16[2048,6144]{1,0:T(8,128)(2,1)}), bf16[512,6144]{1,0:T(8,128)(2,1)}) %reduce-scatter.11.cloned.1.call-update) | async-done | bytes 6291472 | tf_op jit(solution)/shard_map/reduce_scatter | solution.py:315
  2042.0 393.1 %reduce-scatter.15.cloned.1.call-done = bf16[512,11264]{1,0:T(8,128)(2,1)} async-done(((bf16[2048,11264]{1,0:T(8,128)(2,1)}), bf16[512,11264]{1,0:T(8,128)(2,1)}) %reduce-scatter.15.cloned.1.call-update) | async-done | bytes 11534352 | tf_op jit(solution)/shard_map/reduce_scatter | solution.py:239
  2437.7 14.1 fusion.50
  2453.8 14.3 multiply_reduce_fusion.1
  2468.1 15.4 all-reduce.8
  2484.0 15.0 all-reduce.6
  2506.3 432.8 %all-reduce.11.cloned.1.call-done = (bf16[512,6144]{1,0:T(8,128)(2,1)}, bf16[512,2048]{1,0:T(8,128)(2,1)}, bf16[512,11264]{1,0:T(8,128)(2,1)}, bf16[1408,2048]{1,0:T(8,128)(2,1)}) async-done(((bf16[512,6144]{1,0:T(8,128)(2,1)}, bf16[512,2048]{1,0:T(8,128)(2,1)}, bf16[512,11264]{1,0:T(8,128)(2,1)}, bf16[1408,2048]{1,0:T(8,128)(2,1)}), (bf16[512,6144]{1,0:T(8,128)(2,1)}, bf16[512,2048]{1,0:T(8,128)(2,1)}, ...) | async-done | bytes 25690128 | tf_op jit(solution)/shard_map/psum | solution.py:332
  2939.1 10.1 convert_element_type.234
  2951.9 8.3 convert_element_type.244
  2960.1 6.0 convert_element_type.246
  (275 shorter events, 246.0 us)
Async XLA Ops:
  7.2 10.4 copy-start.36
  7.2 18.5 copy-start.32
  7.2 26.2 copy-start
  7.2 233.1 %all-gather.12.cloned.1.call-start = ((), (), s32[]{:S(2)}) async-start(), calls=%async_computation.6 | async-start | bytes 31457280 | tf_op jit(solution)/shard_map/all_gather | solution.py:158
  8.0 330.2 %all-gather.14.cloned.1.call-start = ((), (), s32[]{:S(2)}) async-start(), calls=%async_computation.7 | async-start | bytes 9437184 | tf_op jit(solution)/shard_map/all_gather | solution.py:186
  25.7 226.2 %copy-start.25 = (f32[4,1,512]{2,1,0:T(1,128)}, f32[4,1,512]{2,1,0:T(1,128)S(1)}, u32[]{:S(2)}) copy-start(f32[4,1,512]{2,1,0:T(1,128)S(1)} %convert_element_type.248) | copy-start | bytes 24580
  33.7 218.3 %copy-start.28 = (f32[256]{0:T(256)}, f32[256]{0:T(256)S(1)}, u32[]{:S(2)}) copy-start(f32[256]{0:T(256)S(1)} %get-tuple-element.483) | copy-start | bytes 3076
  34.1 217.8 %copy-start.30 = (f32[256]{0:T(256)}, f32[256]{0:T(256)S(1)}, u32[]{:S(2)}) copy-start(f32[256]{0:T(256)S(1)} %rsqrt_bitcast_fusion) | copy-start | bytes 3076
  34.6 217.3 %copy-start.15 = (bf16[256,2048]{1,0:T(8,128)(2,1)}, bf16[256,2048]{1,0:T(8,128)(2,1)S(1)}, u32[]{:S(2)}) copy-start(bf16[256,2048]{1,0:T(8,128)(2,1)S(1)} %add_convert_fusion.1) | copy-start | bytes 3145732
  251.9 2.7 copy-start.17
  255.8 165.5 %all-gather.16.cloned.1.call-start = ((), (), s32[]{:S(2)}) async-start(), calls=%async_computation.8 | async-start | bytes 9437184 | tf_op jit(solution)/shard_map/all_gather | solution.py:185
  256.7 10.3 copy-start.23
  269.4 239.3 %all-gather.18.cloned.1.call-start = ((), (), s32[]{:S(2)}) async-start(), calls=%async_computation.9 | async-start | bytes 10485760 | tf_op jit(solution)/shard_map/all_gather | solution.py:159
  270.0 642.5 %all-gather.20.cloned.1.call-start = ((), (), s32[]{:S(2)}) async-start(), calls=%async_computation.10 | async-start | bytes 57671680 | tf_op jit(solution)/shard_map/all_gather | solution.py:204
  270.6 8.9 copy-start.38
  270.6 16.0 copy-start.41
  270.6 853.9 %all-gather.22.cloned.1.call-start = ((), (), s32[]{:S(2)}) async-start(), calls=%async_computation.11 | async-start | bytes 28835840 | tf_op jit(solution)/shard_map/all_gather | solution.py:205
  271.2 1158.9 %reduce-scatter.7.cloned.1.call-start = ((), (), s32[]{:S(2)}) async-start(), calls=%async_computation.12 | async-start | bytes 9437184 | tf_op jit(solution)/shard_map/reduce_scatter | solution.py:280
  279.5 633.0 %copy-start.21 = (f32[4,1,512]{2,1,0:T(1,128)}, f32[4,1,512]{2,1,0:T(1,128)S(1)}, u32[]{:S(2)}) copy-start(f32[4,1,512]{2,1,0:T(1,128)S(1)} %convert_element_type.252) | copy-start | bytes 24580
  493.6 15.1 copy-start.2
  493.6 15.1 copy-start.11
  912.5 212.1 %copy-start.18 = (bf16[1,2,128,2048]{3,2,1,0:T(8,128)(2,1)S(1)}, bf16[1,2,128,2048]{3,2,1,0:T(8,128)(2,1)}, u32[]{:S(2)}) copy-start(bf16[1,2,128,2048]{3,2,1,0:T(8,128)(2,1)} %param.27) | copy-start | bytes 3145732
  1176.4 9.1 copy-start.3
  1340.4 180.0 %reduce-scatter.9.cloned.1.call-start = ((), (), s32[]{:S(2)}) async-start(), calls=%async_computation.13 | async-start | bytes 9437184 | tf_op jit(solution)/shard_map/reduce_scatter | solution.py:286
  1341.2 267.7 %reduce-scatter.13.cloned.1.call-start = ((), (), s32[]{:S(2)}) async-start(), calls=%async_computation.15 | async-start | bytes 10485760 | tf_op jit(solution)/shard_map/reduce_scatter | solution.py:321
  1348.7 468.4 %reduce-scatter.17.cloned.1.call-start = ((), (), s32[]{:S(2)}) async-start(), calls=%async_computation.17 | async-start | bytes 28835840 | tf_op jit(solution)/shard_map/reduce_scatter | solution.py:242
  1363.4 678.6 %reduce-scatter.11.cloned.1.call-start = ((), (), s32[]{:S(2)}) async-start(), calls=%async_computation.14 | async-start | bytes 31457280 | tf_op jit(solution)/shard_map/reduce_scatter | solution.py:315
  1430.1 2.6 copy-start.12
  1432.7 89.3 %copy-start.24 = (f32[256,8]{0,1:T(8,128)S(1)}, f32[256,8]{0,1:T(8,128)}, u32[]{:S(2)}) copy-start(f32[256,8]{0,1:T(8,128)} %copy-done.23) | copy-start | bytes 24580
  1432.7 89.3 %copy-start.27 = (f32[256,8]{0,1:T(8,128)S(1)}, f32[256,8]{0,1:T(8,128)}, u32[]{:S(2)}) copy-start(f32[256,8]{0,1:T(8,128)} %get-tuple-element.480) | copy-start | bytes 24580
  1520.4 3.6 copy-start.14
  1521.9 5.1 copy-start.4
  1522.0 3.6 copy-start.13
  1540.8 894.4 %reduce-scatter.15.cloned.1.call-start = ((), (), s32[]{:S(2)}) async-start(), calls=%async_computation.16 | async-start | bytes 57671680 | tf_op jit(solution)/shard_map/reduce_scatter | solution.py:239
  1563.1 1375.9 %all-reduce.11.cloned.1.call-start = ((), (), s32[]{:S(2)}) async-start(), calls=%async_computation.18 | async-start | bytes 51380224 | tf_op jit(solution)/shard_map/psum | solution.py:332
  2437.7 14.1 copy-start.5
  2437.7 14.1 copy-start.7
  2437.7 14.1 copy-start.8
  2451.8 1.9 copy-start.6
  2451.9 1.9 copy-start.26
  2451.9 1.9 copy-start.29
  2451.9 1.9 copy-start.31
  2453.8 14.4 copy-start.33
  2453.8 14.4 copy-start.34
  2939.1 10.1 copy-start.20
  2939.1 12.8 copy-start.10
  2949.2 10.9 slice-start
  2951.9 8.3 slice-start.1
  (9 other events, 10.1 us)
Sparse Core Ops, SparseCore 0:
  9.9 230.3 all-gather.11
  255.9 82.1 all-gather.13
  340.3 80.9 all-gather.15
  423.0 85.6 all-gather.17
  510.4 401.9 all-gather.19
  914.2 210.3 all-gather.21
  1340.5 89.5 reduce-scatter.6
  1432.4 88.0 reduce-scatter.8
  1524.1 84.7 reduce-scatter.12
  1612.4 204.7 reduce-scatter.16
  1820.3 221.6 reduce-scatter.10
  2045.0 390.0 reduce-scatter.14
  2438.0 500.9 all-reduce.10
where the time goes:
time: 2980 us; the launch traced here: 2970 us
  waiting for transfers between devices  2370 us (80%)
  matrix products  376 us (13%)
  blocking collectives  80.8 us (3%)
  other arithmetic  76.8 us (3%)
  local copies, waits for them, and re-layouts  51.8 us (2%)
    psum x1, waiting for transfers between devices, local(): lax.psum(attn_shards[0].astype(jnp.bfloat16), 'ctx').astype(jnp.float32)  433 us
    all_gather x1, waiting for transfers between devices, local(): lax.all_gather(w_gateup, 'dp', axis=0, tiled=True)  397 us
    reduce_scatter x1, waiting for transfers between devices, local(): lax.psum_scatter(grad_gateup.astype(jnp.bfloat16), 'dp', scatter_dimensio...  393 us
    reduce_scatter x1, waiting for transfers between devices, local(): lax.psum_scatter(grad_wqkv.astype(jnp.bfloat16), 'dp', scatter_dimension=...  225 us
    reduce_scatter x1, waiting for transfers between devices, local(): lax.psum_scatter(grad_down.astype(jnp.bfloat16), 'dp', scatter_dimension=...  208 us
    all_gather x1, waiting for transfers between devices, local(): lax.all_gather(w_qkv, 'dp', axis=0, tiled=True)  206 us
    all_gather x1, waiting for transfers between devices, local(): lax.all_gather(w_down, 'dp', axis=0, tiled=True)  184 us
    reduce_scatter x1, waiting for transfers between devices, local(): lax.psum_scatter(grad_values_all.reshape(seq_rows, model_width).astype(jn...  86.1 us
  transfers between devices with their start and end apart: 13, of which 13 were waited for; matrix products, arithmetic and copies ran while one was open for 8% of the time, Pallas kernels for 0%

commit v1 on v0

--- a/solution.py
+++ b/solution.py
@@ -7,6 +7,28 @@
 HEAD_DIM = 64
 ROT = 16
 epsilon = 1e-05
+
+
+def in_order(blocks, dim):
+    blocks = jnp.moveaxis(blocks, 0, dim)
+    shape = blocks.shape
+    return blocks.reshape(*shape[:dim], shape[dim] * shape[dim + 1], *shape[dim + 2 :])
+
+
+def gather_around(x, axis, dim):
+    size = lax.axis_size(axis)
+    pairs = [(i, (i + 1) % size) for i in range(size)]
+    back = [(b, a) for a, b in pairs]
+    lower, upper = ([], [])
+    for step in range(size - 1):
+        if step % 2 == 0:
+            lower.append(lax.ppermute(lower[-1] if lower else x, axis, pairs))
+        else:
+            upper.append(lax.ppermute(upper[-1] if upper else x, axis, back))
+    pieces = jnp.stack([*lower[::-1], x, *upper])
+    shift = lax.axis_index(axis) - len(lower)
+    pieces = pieces[(jnp.arange(size) - shift) % size]
+    return in_order(pieces, dim)
 
 
 def layer_norm(token_rows, gain_vec, shift_vec):
@@ -155,7 +177,7 @@
     cosine, sine_part = rotary_tables(local_pos)
     head_shape = (tok_count, HEADS, HEAD_DIM)
     full_qkv, full_out, gain_one, shift_one, bias_full = (
-        lax.all_gather(w_qkv, "dp", axis=0, tiled=True),
+        gather_around(w_qkv, "dp", 0),
         lax.all_gather(w_out, "dp", axis=0, tiled=True),
         lax.all_gather(first_gain.astype(jnp.bfloat16), "dp", axis=0, tiled=True).astype(
             first_gain.dtype

time: 2980 us -> 3490 us (1.17)
  blocking collectives: 80.8 us -> 343 us
  waiting for transfers between devices: 2370 us -> 2520 us
  other arithmetic: 76.8 us -> 123 us
  local copies, waits for them, and re-layouts: 51.8 us -> 96.5 us
    all_gather x1, blocking collectives: 9.57 us -> 269 us  [local(): lax.all_gather(first_shift.astype(jnp.bfloat16), 'dp', axis=0, tiled=True)]
    ppermute x0 -> x3, waiting for transfers between devices: none -> 137 us  [the longest x2 137 us: gather_around(): lower.append(lax.ppermute(lower[-1] if lower else x, axis, pairs))]
    gather x0 -> x5, local copies, waits for them, and re-layouts: none -> 43.7 us  [gather_around(): pieces = pieces[(jnp.arange(size) - shift) % size]]
  transfers between devices with their start and end apart: 13 -> 16, of which waited for: 13 -> 14; matrix products, arithmetic and copies ran while one was open for 8% -> 7% of each run, Pallas kernels for 0% -> 0%
where the time goes in v1:
time: 3490 us; the launch traced here: 3480 us
  waiting for transfers between devices  2520 us (72%)
  matrix products  370 us (11%)
  blocking collectives  343 us (10%)
  other arithmetic  123 us (4%)
  local copies, waits for them, and re-layouts  96.5 us (3%)
    psum x1, waiting for transfers between devices, local(): lax.psum(attn_shards[0].astype(jnp.bfloat16), 'ctx').astype(jnp.float32)  448 us
    all_gather x1, waiting for transfers between devices, local(): lax.all_gather(w_gateup, 'dp', axis=0, tiled=True)  397 us
    reduce_scatter x1, waiting for transfers between devices, local(): lax.psum_scatter(grad_gateup.astype(jnp.bfloat16), 'dp', scatter_dimensio...  393 us
    all_gather x1, blocking collectives, local(): lax.all_gather(first_shift.astype(jnp.bfloat16), 'dp', axis=0, tiled=True)  269 us
    reduce_scatter x1, waiting for transfers between devices, local(): lax.psum_scatter(grad_wqkv.astype(jnp.bfloat16), 'dp', scatter_dimension=...  225 us
    all_gather x1, waiting for transfers between devices, local(): lax.all_gather(w_qkv, 'dp', axis=0, tiled=True)  220 us
    reduce_scatter x1, waiting for transfers between devices, local(): lax.psum_scatter(grad_down.astype(jnp.bfloat16), 'dp', scatter_dimension=...  208 us
    all_gather x1, waiting for transfers between devices, local(): lax.all_gather(w_down, 'dp', axis=0, tiled=True)  184 us
  transfers between devices with their start and end apart: 16, of which 14 were waited for; matrix products, arithmetic and copies ran while one was open for 7% of the time, Pallas kernels for 0%

profile of v1, /device:TPU:0, one launch (start us, length us, event | category | flops | bytes accessed | tf_op | source)
XLA Modules:
  0.0 3476.3 jit_solution(16995201065497515441)
XLA Ops:
  11.3 136.6 %collective-permute-done = bf16[512,6144]{1,0:T(8,128)(2,1)} collective-permute-done((bf16[512,6144]{1,0:T(8,128)(2,1)}, bf16[512,6144]{1,0:T(8,128)(2,1)}, u32[]{:S(2)}, u32[]{:S(2)}) %collective-permute-start) | collective-permute-done | bytes 6291488 | tf_op jit(solution)/shard_map/ppermute | solution.py:25
  149.6 269.4 %all-gather.1 = bf16[4,1,512]{2,1,0:T(2,128)(2,1)S(1)} all-gather(bf16[1,1,512]{2,1,0:T(2,128)(2,1)S(1)} %reshape.419), channel_id=1, replica_groups=mesh['dp'=4,'ctx'=8] {'dp'}, dimensions={0}, use_global_device_ids=true | all-gather | bytes 5120 | tf_op jit(solution)/shard_map/all_gather | solution.py:185
  419.8 8.1 all-gather
  428.6 7.2 all-gather.2
  441.8 20.8 pad_maximum_fusion
  462.6 17.9 fusion.66
  480.5 6.4 gather_fusion.3
  486.9 6.4 gather_fusion.2
  493.4 6.4 gather_fusion.1
  499.8 6.4 gather_fusion
  506.2 17.4 pad_maximum_fusion.1
  523.7 11.6 convolution_add_fusion
  554.9 8.3 all-gather.4
  563.2 6.9 all-gather.3
  571.5 12.3 all-reduce
  585.5 36.3 %all-gather.12.cloned.1.call-done = bf16[2048,2048]{1,0:T(8,128)(2,1)} async-done(((bf16[256,2048]{1,0:T(8,128)(2,1)}), bf16[2048,2048]{1,0:T(8,128)(2,1)}) %all-gather.12.cloned.1.call-update) | async-done | bytes 8388624 | tf_op jit(solution)/shard_map/all_gather | solution.py:208
  621.8 12.3 copy.38
  634.1 70.9 %all-gather.14.cloned.1.call-done = bf16[2048,2048]{0,1:T(8,128)(2,1)} async-done(((bf16[256,2048]{0,1:T(8,128)(2,1)}), bf16[2048,2048]{0,1:T(8,128)(2,1)}) %all-gather.14.cloned.1.call-update) | async-done | bytes 8388624 | tf_op jit(solution)/shard_map/all_gather | solution.py:207
  705.1 72.2 %while.34 = (s32[]{:T(128)}, bf16[256,32,64]{0,2,1:T(8,128)(2,1)S(1)}, f32[32,256]{1,0:T(8,128)S(1)}, bf16[2048,32,64]{0,2,1:T(8,128)(2,1)}, bf16[256,32,64]{0,2...) while((s32[]{:T(128)}, ...), condition=%wide.region_5.6_spmd.clone, body=%wide.region_2.5_spmd.clone.sunk | while | flops 560528384 | bytes 29666480 | solution.py:101
  777.4 15.1 all-gather.16.cloned.1.call-done
  792.6 6.2 fusion.68
  799.1 397.2 %all-gather.18.cloned.1.call-done = bf16[2048,11264]{1,0:T(8,128)(2,1)} async-done(((bf16[512,11264]{1,0:T(8,128)(2,1)}), bf16[2048,11264]{1,0:T(8,128)(2,1)}) %all-gather.18.cloned.1.call-update) | async-done | bytes 46137360 | tf_op jit(solution)/shard_map/all_gather | solution.py:226
  1196.3 28.4 fusion.65
  1224.7 183.7 %all-gather.20.cloned.1.call-done = bf16[5632,2048]{1,0:T(8,128)(2,1)} async-done(((bf16[1408,2048]{1,0:T(8,128)(2,1)}), bf16[5632,2048]{1,0:T(8,128)(2,1)}) %all-gather.20.cloned.1.call-update) | async-done | bytes 23068688 | tf_op jit(solution)/shard_map/all_gather | solution.py:227
  1408.4 26.0 multiply_convert_fusion.2
  1434.4 22.2 multiply_reduce_fusion
  1460.5 5.8 convolution_convert_fusion.4
  1476.8 137.2 %while.35 = (s32[]{:T(128)}, f32[256,32,64]{0,2,1:T(8,128)S(1)}, bf16[2048,32,64]{0,2,1:T(8,128)(2,1)}, bf16[2048,32,64]{0,2,1:T(8,128)(2,1)}, bf16[2048,32,64]{...) while((s32[]{:T(128)}, f32[256,32,64]{0,2,1:T(8,128)S(1)}, ...), condition=%wide.region_11.12_spmd.clone, body=%wide.region_10.11_spmd.clone.sunk | while | flops 1364262912 | bytes 47491280 | solution.py:154
  1480.0 4.5 multiply_convert_fusion.5
  1617.0 5.8 convolution_convert_fusion.3
  1624.6 12.9 convolution_convert_fusion.1
  1640.4 63.4 %reduce-scatter.7.cloned.1.call-done = bf16[256,2048]{0,1:T(8,128)(2,1)} async-done(((bf16[2048,2048]{0,1:T(8,128)(2,1)}), bf16[256,2048]{0,1:T(8,128)(2,1)}) %reduce-scatter.7.cloned.1.call-update) | async-done | bytes 1048592 | tf_op jit(solution)/shard_map/reduce_scatter | solution.py:302
  1709.0 85.0 %reduce-scatter.9.cloned.1.call-done = bf16[256,2048]{0,1:T(8,128)(2,1)} async-done(((bf16[2048,2048]{0,1:T(8,128)(2,1)}), bf16[256,2048]{0,1:T(8,128)(2,1)}) %reduce-scatter.9.cloned.1.call-update) | async-done | bytes 1048592 | tf_op jit(solution)/shard_map/reduce_scatter | solution.py:308
  1802.2 219.8 %all-gather.22.cloned.1.call-done = bf16[2048,6144]{1,0:T(8,128)(2,1)} async-done(((bf16[512,6144]{1,0:T(8,128)(2,1)}), bf16[2048,6144]{1,0:T(8,128)(2,1)}) %all-gather.22.cloned.1.call-update) | async-done | bytes 25165840 | tf_op jit(solution)/shard_map/all_gather | solution.py:281
  2022.0 15.7 multiply_reduce_fusion.1
  2037.7 13.9 convolution_convert_fusion.2
  2053.3 22.4 convolution_convert_fusion
  2075.8 36.2 %reduce-scatter.13.cloned.1.call-done = bf16[512,2048]{1,0:T(8,128)(2,1)} async-done(((bf16[2048,2048]{1,0:T(8,128)(2,1)}), bf16[512,2048]{1,0:T(8,128)(2,1)}) %reduce-scatter.13.cloned.1.call-update) | async-done | bytes 2097168 | tf_op jit(solution)/shard_map/reduce_scatter | solution.py:343
  2112.0 208.3 %reduce-scatter.17.cloned.1.call-done = bf16[1408,2048]{1,0:T(8,128)(2,1)} async-done(((bf16[5632,2048]{1,0:T(8,128)(2,1)}), bf16[1408,2048]{1,0:T(8,128)(2,1)}) %reduce-scatter.17.cloned.1.call-update) | async-done | bytes 5767184 | tf_op jit(solution)/shard_map/reduce_scatter | solution.py:264
  2320.3 224.9 %reduce-scatter.11.cloned.1.call-done = bf16[512,6144]{1,0:T(8,128)(2,1)} async-done(((bf16[2048,6144]{1,0:T(8,128)(2,1)}), bf16[512,6144]{1,0:T(8,128)(2,1)}) %reduce-scatter.11.cloned.1.call-update) | async-done | bytes 6291472 | tf_op jit(solution)/shard_map/reduce_scatter | solution.py:337
  2545.1 393.1 %reduce-scatter.15.cloned.1.call-done = bf16[512,11264]{1,0:T(8,128)(2,1)} async-done(((bf16[2048,11264]{1,0:T(8,128)(2,1)}), bf16[512,11264]{1,0:T(8,128)(2,1)}) %reduce-scatter.15.cloned.1.call-update) | async-done | bytes 11534352 | tf_op jit(solution)/shard_map/reduce_scatter | solution.py:261
  2940.8 13.9 fusion.50
  2956.5 15.4 all-reduce.8
  2972.3 15.0 all-reduce.6
  2994.1 448.1 %all-reduce.11.cloned.1.call-done = (bf16[512,6144]{1,0:T(8,128)(2,1)}, bf16[512,2048]{1,0:T(8,128)(2,1)}, bf16[512,11264]{1,0:T(8,128)(2,1)}, bf16[1408,2048]{1,0:T(8,128)(2,1)}) async-done(((bf16[512,6144]{1,0:T(8,128)(2,1)}, bf16[512,2048]{1,0:T(8,128)(2,1)}, bf16[512,11264]{1,0:T(8,128)(2,1)}, bf16[1408,2048]{1,0:T(8,128)(2,1)}), (bf16[512,6144]{1,0:T(8,128)(2,1)}, bf16[512,2048]{1,0:T(8,128)(2,1)}, ...) | async-done | bytes 25690128 | tf_op jit(solution)/shard_map/psum | solution.py:354
  3442.1 10.2 convert_element_type.242
  3455.0 8.3 convert_element_type.252
  3463.3 6.0 convert_element_type.254
  (305 shorter events, 289.6 us)
Async XLA Ops:
  7.2 614.6 %all-gather.12.cloned.1.call-start = ((), (), s32[]{:S(2)}) async-start(), calls=%async_computation.6 | async-start | bytes 9437184 | tf_op jit(solution)/shard_map/all_gather | solution.py:208
  7.2 140.7 %collective-permute-start = (bf16[512,6144]{1,0:T(8,128)(2,1)}, bf16[512,6144]{1,0:T(8,128)(2,1)}, u32[]{:S(2)}, u32[]{:S(2)}) collective-permute-start(bf16[512,6144]{1,0:T(8,128)(2,1)} %param.20), channel_id=1, source_target_pairs={{0,8},{8,16},{16,24},{24,0},{1,9},{9,17},{17,25},{25,1},{2,10},{10... | collective-permute-start | bytes 18874376 | tf_op jit(solution)/shard_map/ppermute | solution.py:25
  10.2 431.5 %collective-permute-start.2 = (bf16[512,6144]{1,0:T(8,128)(2,1)}, bf16[512,6144]{1,0:T(8,128)(2,1)}, u32[]{:S(2)}, u32[]{:S(2)}) collective-permute-start(bf16[512,6144]{1,0:T(8,128)(2,1)} %param.20), channel_id=1, source_target_pairs={{8,0},{16,8},{24,16},{0,24},{9,1},{17,9},{25,17},{1,25},{10,2},{18... | collective-permute-start | bytes 18874376 | tf_op jit(solution)/shard_map/ppermute | solution.py:27
  147.9 293.9 %collective-permute-start.1 = (bf16[512,6144]{1,0:T(8,128)(2,1)}, bf16[512,6144]{1,0:T(8,128)(2,1)}, u32[]{:S(2)}, u32[]{:S(2)}) collective-permute-start(bf16[512,6144]{1,0:T(8,128)(2,1)} %collective-permute-done), channel_id=1, source_target_pairs={{0,8},{8,16},{16,24},{24,0},{1,9},{9,17},{17,25},{25,1},{2,10},{10... | collective-permute-start | bytes 18874376 | tf_op jit(solution)/shard_map/ppermute | solution.py:25
  419.1 43.5 %copy-start.35 = (f32[4,1,512]{2,1,0:T(1,128)}, f32[4,1,512]{2,1,0:T(1,128)S(1)}, u32[]{:S(2)}) copy-start(f32[4,1,512]{2,1,0:T(1,128)S(1)} %convert_element_type.257) | copy-start | bytes 24580
  427.9 34.7 copy-start.32
  523.7 15.5 copy-start.43
  539.2 165.8 %all-gather.14.cloned.1.call-start = ((), (), s32[]{:S(2)}) async-start(), calls=%async_computation.7 | async-start | bytes 9437184 | tf_op jit(solution)/shard_map/all_gather | solution.py:207
  540.0 10.4 copy-start.30
  552.9 239.7 %all-gather.16.cloned.1.call-start = ((), (), s32[]{:S(2)}) async-start(), calls=%async_computation.8 | async-start | bytes 10485760 | tf_op jit(solution)/shard_map/all_gather | solution.py:181
  553.6 642.7 %all-gather.18.cloned.1.call-start = ((), (), s32[]{:S(2)}) async-start(), calls=%async_computation.9 | async-start | bytes 57671680 | tf_op jit(solution)/shard_map/all_gather | solution.py:226
  554.2 9.0 copy-start.42
  554.2 15.9 copy-start.45
  554.2 854.1 %all-gather.20.cloned.1.call-start = ((), (), s32[]{:S(2)}) async-start(), calls=%async_computation.10 | async-start | bytes 28835840 | tf_op jit(solution)/shard_map/all_gather | solution.py:227
  554.8 1148.9 %reduce-scatter.7.cloned.1.call-start = ((), (), s32[]{:S(2)}) async-start(), calls=%async_computation.11 | async-start | bytes 9437184 | tf_op jit(solution)/shard_map/reduce_scatter | solution.py:302
  563.2 633.1 %copy-start.24 = (f32[4,1,512]{2,1,0:T(1,128)}, f32[4,1,512]{2,1,0:T(1,128)S(1)}, u32[]{:S(2)}) copy-start(f32[4,1,512]{2,1,0:T(1,128)S(1)} %convert_element_type.260) | copy-start | bytes 24580
  570.2 886.5 %copy-start.22 = (f32[4,1,512]{2,1,0:T(1,128)}, f32[4,1,512]{2,1,0:T(1,128)S(1)}, u32[]{:S(2)}) copy-start(f32[4,1,512]{2,1,0:T(1,128)S(1)} %convert_element_type.259) | copy-start | bytes 24580
  705.1 87.4 %copy-start.2 = (bf16[1,2,128,2048]{3,2,1,0:T(8,128)(2,1)S(1)}, bf16[1,2,128,2048]{3,2,1,0:T(8,128)(2,1)}, u32[]{:S(2)}) copy-start(bf16[1,2,128,2048]{3,2,1,0:T(8,128)(2,1)} %param.16) | copy-start | bytes 3145732
  777.4 15.2 copy-start.4
  777.4 15.2 copy-start.13
  798.7 657.9 %copy-start = (f32[256,2048]{1,0:T(8,128)}, f32[256,2048]{1,0:T(8,128)S(1)}, u32[]{:S(2)}) copy-start(f32[256,2048]{1,0:T(8,128)S(1)} %get-tuple-element.495) | copy-start | bytes 6291460
  798.7 657.9 %copy-start.26 = (f32[256]{0:T(256)}, f32[256]{0:T(256)S(1)}, u32[]{:S(2)}) copy-start(f32[256]{0:T(256)S(1)} %broadcast_multiply_fusion.5) | copy-start | bytes 3076
  799.1 657.6 %copy-start.28 = (f32[256]{0:T(256)}, f32[256]{0:T(256)S(1)}, u32[]{:S(2)}) copy-start(f32[256]{0:T(256)S(1)} %add_rsqrt_fusion) | copy-start | bytes 3076
  1196.3 212.1 %copy-start.19 = (bf16[1,2,128,2048]{3,2,1,0:T(8,128)(2,1)S(1)}, bf16[1,2,128,2048]{3,2,1,0:T(8,128)(2,1)}, u32[]{:S(2)}) copy-start(bf16[1,2,128,2048]{3,2,1,0:T(8,128)(2,1)} %param.27) | copy-start | bytes 3145732
  1614.0 180.0 %reduce-scatter.9.cloned.1.call-start = ((), (), s32[]{:S(2)}) async-start(), calls=%async_computation.12 | async-start | bytes 9437184 | tf_op jit(solution)/shard_map/reduce_scatter | solution.py:308
  1615.4 406.6 %all-gather.22.cloned.1.call-start = ((), (), s32[]{:S(2)}) async-start(), calls=%async_computation.13 | async-start | bytes 31457280 | tf_op jit(solution)/shard_map/all_gather | solution.py:281
  1616.2 495.8 %reduce-scatter.13.cloned.1.call-start = ((), (), s32[]{:S(2)}) async-start(), calls=%async_computation.15 | async-start | bytes 10485760 | tf_op jit(solution)/shard_map/reduce_scatter | solution.py:343
  1622.8 697.4 %reduce-scatter.17.cloned.1.call-start = ((), (), s32[]{:S(2)}) async-start(), calls=%async_computation.17 | async-start | bytes 28835840 | tf_op jit(solution)/shard_map/reduce_scatter | solution.py:264
  1637.5 907.6 %reduce-scatter.11.cloned.1.call-start = ((), (), s32[]{:S(2)}) async-start(), calls=%async_computation.14 | async-start | bytes 31457280 | tf_op jit(solution)/shard_map/reduce_scatter | solution.py:337
  1639.1 156.6 %copy-start.31 = (f32[256,8]{0,1:T(8,128)S(1)}, f32[256,8]{0,1:T(8,128)}, u32[]{:S(2)}) copy-start(f32[256,8]{0,1:T(8,128)} %copy-done.30) | copy-start | bytes 24580
  1639.1 156.6 %copy-start.34 = (f32[256,8]{0,1:T(8,128)S(1)}, f32[256,8]{0,1:T(8,128)}, u32[]{:S(2)}) copy-start(f32[256,8]{0,1:T(8,128)} %get-tuple-element.485) | copy-start | bytes 24580
  1795.6 242.2 %copy-start.6 = (f32[256,2048]{0,1:T(8,128)}, f32[256,2048]{0,1:T(8,128)S(1)}, u32[]{:S(2)}) copy-start(f32[256,2048]{0,1:T(8,128)S(1)} %convert_element_type.234) | copy-start | bytes 6291460
  1795.6 226.4 %copy-start.3 = (bf16[1,2,128,2048]{3,2,1,0:T(8,128)(2,1)S(1)}, bf16[1,2,128,2048]{3,2,1,0:T(8,128)(2,1)}, u32[]{:S(2)}) copy-start(bf16[1,2,128,2048]{3,2,1,0:T(8,128)(2,1)} %param.16) | copy-start | bytes 3145732
  1795.6 226.4 %copy-start.33 = (f32[4,1,512]{2,1,0:T(1,128)S(1)}, f32[4,1,512]{2,1,0:T(1,128)}, u32[]{:S(2)}) copy-start(f32[4,1,512]{2,1,0:T(1,128)} %copy-done.32) | copy-start | bytes 24580
  1795.6 226.4 %copy-start.36 = (f32[4,1,512]{2,1,0:T(1,128)S(1)}, f32[4,1,512]{2,1,0:T(1,128)}, u32[]{:S(2)}) copy-start(f32[4,1,512]{2,1,0:T(1,128)} %copy-done.35) | copy-start | bytes 24580
  1795.6 226.4 %copy-start.39 = (f32[256]{0:T(256)S(1)}, f32[256]{0:T(256)}, u32[]{:S(2)}) copy-start(f32[256]{0:T(256)} %get-tuple-element.490) | copy-start | bytes 3076
  1795.6 226.4 %copy-start.40 = (f32[256]{0:T(256)S(1)}, f32[256]{0:T(256)}, u32[]{:S(2)}) copy-start(f32[256]{0:T(256)} %get-tuple-element.488) | copy-start | bytes 3076
  2051.7 886.5 %reduce-scatter.15.cloned.1.call-start = ((), (), s32[]{:S(2)}) async-start(), calls=%async_computation.16 | async-start | bytes 57671680 | tf_op jit(solution)/shard_map/reduce_scatter | solution.py:261
  2075.7 1366.4 %all-reduce.11.cloned.1.call-start = ((), (), s32[]{:S(2)}) async-start(), calls=%async_computation.18 | async-start | bytes 51380224 | tf_op jit(solution)/shard_map/psum | solution.py:354
  2940.7 13.9 copy-start.7
  2940.8 13.9 copy-start.8
  2940.8 13.9 copy-start.9
  2954.7 35.6 %copy-start.12 = (f32[256,2048]{1,0:T(8,128)S(1)}, f32[256,2048]{1,0:T(8,128)}, u32[]{:S(2)}) copy-start(f32[256,2048]{1,0:T(8,128)} %copy-done.10) | copy-start | bytes 6291460
  3442.1 12.9 slice-start
  3442.1 10.2 copy-start.21
  3442.1 12.9 slice-start.1
  3442.1 12.9 slice-start.2
  3452.3 11.0 slice-start.3
  (19 other events, 43.3 us)
Sparse Core Ops, SparseCore 0:
  539.3 82.4 all-gather.11
  624.0 80.9 all-gather.13
  706.9 85.6 all-gather.15
  794.3 401.9 all-gather.17
  1198.0 210.3 all-gather.19
  1614.2 89.5 reduce-scatter.6
  1706.0 87.9 reduce-scatter.8
  1795.9 226.0 all-gather.21
  2025.6 86.3 reduce-scatter.12
  2115.5 204.7 reduce-scatter.16
  2323.4 221.6 reduce-scatter.10
  2548.1 390.0 reduce-scatter.14
  2941.1 500.9 all-reduce.10
